TPU v7x, 8 devices: a whole 2x2x1 slice. The times are simulated.
8 devices in a mesh: dp: 2 (over z, y), cp: 4 (over x, core).
Axes of the slice: x: 2, y: 2, z: 1, core: 2. Of those that a mesh axis runs over, the one named last changes fastest.
Arguments:
- hidden: bfloat16 [32, 1024, 640], P('dp', 'cp'), parts along dimension 0
- positions: int32 [32, 1024], P('dp', 'cp'), parts along dimension 0
- wq_local: bfloat16 [640, 1024], replicated
- wk_local: bfloat16 [640, 256], replicated
- wv_local: bfloat16 [640, 256], replicated
- wo_local: bfloat16 [1024, 640], replicated
- wgate_local: bfloat16 [640, 2048], replicated
- wup_local: bfloat16 [640, 2048], replicated
- wdown_local: bfloat16 [2048, 640], replicated
- preatt_local: float32 [640], replicated
- postatt_local: float32 [640], replicated
- preffw_local: float32 [640], replicated
- postffw_local: float32 [640], replicated
- wq_global: bfloat16 [640, 1024], replicated
- wk_global: bfloat16 [640, 256], replicated
- wv_global: bfloat16 [640, 256], replicated
- wo_global: bfloat16 [1024, 640], replicated
- wgate_global: bfloat16 [640, 2048], replicated
- wup_global: bfloat16 [640, 2048], replicated
- wdown_global: bfloat16 [2048, 640], replicated
- preatt_global: float32 [640], replicated
- postatt_global: float32 [640], replicated
- preffw_global: float32 [640], replicated
- postffw_global: float32 [640], replicated
Outputs:
- output: bfloat16 [32, 1024, 640], P('dp', 'cp'), parts along dimension 0
There are 2 independent parts. A program takes and returns all parts, laid end to end along the dimension named above; an argument that names none is the same for every part.
All inputs are finite; a program needn't handle non-finite values.
Results may differ from a plain program's by a relative error of at most 0.02.
Values are sent between devices in bfloat16 or wider.
A program may use at most 1 GiB of HBM per device.

v0:
```python
import jax
import jax.numpy as jnp
from jax import lax
from jax.sharding import PartitionSpec as P

HEAD_DIM = 256
WINDOW = 512
EPSILON = 1e-6
THETA = 10000.0
SOFT_CAP = 50.0


def rms_norm(inputs, norm_scale):
    widened = inputs.astype(jnp.float32)
    mean_sq = jnp.mean(widened * widened, axis=-1, keepdims=True)
    return (widened * lax.rsqrt(mean_sq + EPSILON) * (1.0 + norm_scale)).astype(jnp.bfloat16)


def rope_tables(tok_pos):
    half_dim = HEAD_DIM // 2
    inv_freq = THETA ** (-(jnp.arange(half_dim, dtype=jnp.float32) * 2.0 / HEAD_DIM))
    angles = tok_pos.astype(jnp.float32)[:, :, None, None] * inv_freq
    return jnp.cos(angles), jnp.sin(angles)


def apply_rope(heads_in, cos_t, sin_t):
    half_dim = HEAD_DIM // 2
    widened = heads_in.astype(jnp.float32)
    first_half = widened[..., :half_dim]
    second_half = widened[..., half_dim:]
    return jnp.concatenate([first_half * cos_t - second_half * sin_t, second_half * cos_t + first_half * sin_t], axis=-1)


def project_qkv(hidden, cos_t, sin_t, weights):
    w_q, w_k, w_v, pre_att = weights[0], weights[1], weights[2], weights[7]
    batch_rows, tok_len = hidden.shape[0], hidden.shape[1]
    kv_heads = w_k.shape[1] // HEAD_DIM
    group_size = w_q.shape[1] // w_k.shape[1]
    normed = rms_norm(hidden, pre_att)
    q_raw = jnp.einsum("btd,dn->btn", normed, w_q, preferred_element_type=jnp.float32).astype(jnp.bfloat16)
    k_raw = jnp.einsum("btd,dn->btn", normed, w_k, preferred_element_type=jnp.float32).astype(jnp.bfloat16)
    v_raw = jnp.einsum("btd,dn->btn", normed, w_v, preferred_element_type=jnp.float32).astype(jnp.bfloat16)
    query_rot = apply_rope(q_raw.reshape(batch_rows, tok_len, kv_heads * group_size, HEAD_DIM), cos_t, sin_t)
    query_rot = (query_rot * HEAD_DIM ** -0.5).astype(jnp.bfloat16).reshape(batch_rows, tok_len, kv_heads, group_size, HEAD_DIM)
    key_rot = apply_rope(k_raw.reshape(batch_rows, tok_len, kv_heads, HEAD_DIM), cos_t, sin_t).astype(jnp.bfloat16)
    value_t = v_raw.reshape(batch_rows, tok_len, kv_heads, HEAD_DIM)
    return query_rot, key_rot, value_t


def attend(query_rot, key_all, value_all, q_pos, k_pos, window_len):
    scores = jnp.einsum("btkgd,bskd->bkgts", query_rot, key_all, preferred_element_type=jnp.float32)
    capped = SOFT_CAP * jnp.tanh(scores / SOFT_CAP)
    offset = q_pos[:, None, None, :, None] - k_pos[:, None, None, None, :]
    visible = (offset >= 0) & (offset < window_len)
    prob_bf = jax.nn.softmax(jnp.where(visible, capped, -1e30), axis=-1).astype(jnp.bfloat16)
    mixed_heads = jnp.einsum("bkgts,bskd->btkgd", prob_bf, value_all, preferred_element_type=jnp.float32).astype(jnp.bfloat16)
    return mixed_heads.reshape(query_rot.shape[0], query_rot.shape[1], -1)


def finish_layer(hidden, mixed_heads, weights):
    w_o, w_gate, w_up, w_down = weights[3], weights[4], weights[5], weights[6]
    post_att, pre_ffw, post_ffw = weights[8], weights[9], weights[10]
    attn_out = jnp.einsum("btn,nd->btd", mixed_heads, w_o, preferred_element_type=jnp.float32).astype(jnp.bfloat16)
    mid_state = (hidden.astype(jnp.float32) + rms_norm(attn_out, post_att).astype(jnp.float32)).astype(jnp.bfloat16)
    normed_mid = rms_norm(mid_state, pre_ffw)
    gate_val = jnp.einsum("btd,df->btf", normed_mid, w_gate, preferred_element_type=jnp.float32).astype(jnp.bfloat16)
    up_val = jnp.einsum("btd,df->btf", normed_mid, w_up, preferred_element_type=jnp.float32).astype(jnp.bfloat16)
    act_val = (jax.nn.gelu(gate_val.astype(jnp.float32), approximate=True) * up_val.astype(jnp.float32)).astype(jnp.bfloat16)
    down_val = jnp.einsum("btf,fd->btd", act_val, w_down, preferred_element_type=jnp.float32).astype(jnp.bfloat16)
    return (mid_state.astype(jnp.float32) + rms_norm(down_val, post_ffw).astype(jnp.float32)).astype(jnp.bfloat16)


def solution(mesh):
    cp_size = mesh.shape["cp"]

    def device_step(hidden, positions, *weights):
        local_w = weights[:11]
        global_w = weights[11:]
        chunk_len = hidden.shape[1]
        my_index = lax.axis_index("cp")
        all_pos = lax.all_gather(positions, "cp", axis=1, tiled=True)
        cos_t, sin_t = rope_tables(positions)
        n_prev = (WINDOW + chunk_len - 2) // chunk_len
        query_rot, key_rot, value_t = project_qkv(hidden, cos_t, sin_t, local_w)
        key_parts = [key_rot]
        value_parts = [value_t]
        pos_parts = [positions]
        for shift_by in range(1, n_prev + 1):
            perm_pairs = [(source_idx, source_idx + shift_by) for source_idx in range(cp_size - shift_by)]
            key_parts.append(lax.ppermute(key_rot, "cp", perm_pairs))
            value_parts.append(lax.ppermute(value_t, "cp", perm_pairs))
            start_at = ((my_index - shift_by) % cp_size) * chunk_len
            pos_parts.append(lax.dynamic_slice_in_dim(all_pos, start_at, chunk_len, axis=1))
        mixed_heads = attend(query_rot, jnp.concatenate(key_parts, axis=1), jnp.concatenate(value_parts, axis=1), positions, jnp.concatenate(pos_parts, axis=1), WINDOW)
        mid_hidden = finish_layer(hidden, mixed_heads, local_w)
        query_rot, key_rot, value_t = project_qkv(mid_hidden, cos_t, sin_t, global_w)
        key_all = lax.all_gather(key_rot, "cp", axis=1, tiled=True)
        value_all = lax.all_gather(value_t, "cp", axis=1, tiled=True)
        mixed_heads = attend(query_rot, key_all, value_all, positions, all_pos, 2 * chunk_len * cp_size)
        return finish_layer(mid_hidden, mixed_heads, global_w)

    specs_in = tuple([P("dp", "cp"), P("dp", "cp")] + [P()] * 22)
    return jax.shard_map(device_step, mesh=mesh, in_specs=specs_in, out_specs=P("dp", "cp"), check_vma=False)
```

profile of v0, /device:TPU:3, one launch (start us, length us, event | category | flops | bytes accessed | tf_op | source)
XLA Modules:
  0.0 670.9 jit_solution(18122649593073631782)
XLA Ops:
  6.6 0.8 broadcast_add_fusion.7
  7.4 3.6 fusion.48
  11.0 0.9 convert_element_type.221
  11.9 4.6 bitcast_convert_fusion.1
  16.5 8.6 %fusion.135 = (bf16[16,256,1,128]{1,3,0,2:T(8,128)(2,1)S(1)}, bf16[16,256,1,128]{1,3,0,2:T(8,128)(2,1)S(1)}) fusion(f32[16,256,1,256]{1,3,0,2:T(8,128)S(1)} %bitcast_convert_fusion.1, f32[128]{0:T(128)S(1)} %negate_power_fusion, f32[16,256]{1,0:T(8,128)S(1)} %convert_element_type.221), kind=kLoop, calls=%fused_computation.155 | loop fusion | flops 4718592 | bytes 6308352 | tf_op jit(solution)/shard_map/convert.6
  25.1 1.0 copy-done.8
  26.1 1.5 pad_maximum_fusion
  27.6 1.4 collective-permute-start.3
  29.0 1.3 collective-permute-start.2
  30.4 3.2 convert_bitcast_fusion
  33.6 1.3 collective-permute-start.1
  34.9 1.3 collective-permute-start
  36.2 132.2 %all_gather.9 = s32[16,1024]{1,0:T(8,128)S(1)} all-gather(s32[16,256]{1,0:T(8,128)S(1)} %copy-done.12), channel_id=1, replica_groups=mesh['dp'=2,'cp'=4] {'cp'}, dimensions={1}, use_global_device_ids=true | all-gather | bytes 81920 | tf_op jit(solution)/shard_map/all_gather | solution.py:81
  168.5 8.8 %multiply_cosine_fusion = (f32[16,256,128]{2,1,0:T(8,128)}, f32[16,256,128]{2,1,0:T(8,128)}) fusion(f32[128]{0:T(128)S(1)} %negate_power_fusion, f32[16,256]{1,0:T(8,128)S(1)} %convert_element_type.221), kind=kLoop, calls=%fused_computation.133 | loop fusion | flops 524288 | bytes 4211200 | tf_op jit(solution)/shard_map/cos | solution.py:23
  178.5 13.0 %convert_convert_fusion.1 = f32[16,256,1024]{2,1,0:T(8,128)} fusion(bf16[16,256,640]{2,1,0:T(8,128)(2,1)} %param.24, f32[640]{0:T(1024)S(1)} %broadcast_add_fusion.7, f32[16,256]{1,0:T(8,128)S(1)} %add_rsqrt_fusion.7, bf16[640,1024]{1,0:T(8,128)(2,1)} %param.26), kind=kOutput, calls=%fused_computation.111 | convolution fusion | flops 5387583488 | bytes 23349760 | tf_op jit(solution)/shard_map/btd,dn->btn/dot_general | solution.py:40
  191.5 20.4 %reshape.287 = f32[16,256,4,256]{3,2,1,0:T(4,128)} reshape(f32[16,256,1024]{2,1,0:T(8,128)} %convert_convert_fusion.1) | data formatting | bytes 33554432 | tf_op jit(solution)/shard_map/convert_element_type | solution.py:28
  211.9 11.4 %fusion.183 = (f32[16,256,4,128]{3,2,1,0:T(4,128)}, f32[16,256,4,128]{3,2,1,0:T(4,128)}) fusion(f32[16,256,4,256]{3,2,1,0:T(4,128)} %reshape.287), kind=kLoop, calls=%fused_computation.217 | loop fusion | bytes 33554432 | tf_op jit(solution)/shard_map/slice | solution.py:29
  224.4 5.1 fusion.31
  229.6 12.4 %multiply_subtract_fusion.1 = (f32[16,256,4,128]{3,1,2,0:T(8,128)}, f32[16,256,4,128]{3,1,2,0:T(8,128)}) fusion(f32[16,256,4,128]{3,2,1,0:T(4,128)} %get-tuple-element.18, f32[16,256,4,128]{3,2,1,0:T(4,128)} %get-tuple-element.17, f32[16,256,128]{2,1,0:T(8,128)} %get-tuple-element.26, f32[16,256,128]{2,1,0:T(8,128)} %get-tuple-element.25), kind=kLoop, calls=%fused_computation.110 | loop fusion | flops 12582912 | bytes 37748736 | tf_op jit(solution)/shard_map/sub | solution.py:31
  242.0 29.3 %fusion.20 = (f32[16,4,256]{2,1,0:T(4,128)S(1)}, f32[16,768,256,4]{2,1,3,0:T(8,128)}) fusion(pred[16,256,768]{1,2,0:T(8,128)(4,1)} %fusion.31, f32[16,256,4,128]{3,1,2,0:T(8,128)} %get-tuple-element.14, f32[16,256,4,128]{3,1,2,0:T(8,128)} %get-tuple-element.13, bf16[16,256,1,256]{1,3,0,2:T(8,128)(2,1)} %collective-permute-done.3, ...), kind=kOutput, calls=%fused_computation.34 | convolution fusion | flops 6530514944 | bytes 76611584 | tf_op jit(solution)/shard_map/btkgd,bskd->bkgts/dot_general | solution.py:51
  271.3 24.1 %fusion.1 = f32[16,4,256]{2,1,0:T(4,128)S(1)} fusion(f32[16,768,256,4]{2,1,3,0:T(8,128)} %get-tuple-element.28, f32[16,4,256]{2,1,0:T(4,128)S(1)} %get-tuple-element.27, pred[16,256,768]{1,2,0:T(8,128)(4,1)} %fusion.31), kind=kLoop, calls=%fused_computation.15 | loop fusion | flops 62898176 | bytes 53608448 | tf_op jit(solution)/shard_map/reduce_sum | solution.py:55
  295.4 27.4 %fusion.72 = bf16[16,256,4,256]{3,1,2,0:T(8,128)(2,1)} fusion(f32[16,4,256]{2,1,0:T(4,128)S(1)} %fusion.1, f32[16,4,256]{2,1,0:T(4,128)S(1)} %get-tuple-element.27, f32[16,768,256,4]{2,1,3,0:T(8,128)} %get-tuple-element.28, pred[16,256,768]{1,2,0:T(8,128)(4,1)} %fusion.31, bf16[16,256,1,256]{3,1,0,2:T(8,128)(2,1)} %collective-permute-done.1, ...), kind=kOutput, calls=%fused_computation.112 | convolution fusion | flops 6541017088 | bytes 68288512 | tf_op jit(solution)/shard_map/bkgts,bskd->btkgd/dot_general | solution.py:56
  322.8 10.1 %fusion.36 = (f32[16,256]{1,0:T(8,128)S(1)}, bf16[16,256,640]{2,1,0:T(8,128)(2,1)S(1)}) fusion(bf16[16,256,1024]{1,2,0:T(8,128)(2,1)} %bitcast.152, bf16[1024,640]{1,0:T(8,128)(2,1)} %param.29), kind=kOutput, calls=%fused_computation.72 | convolution fusion | flops 5379190784 | bytes 14958592 | tf_op jit(solution)/shard_map/btn,nd->btd/dot_general | solution.py:63
  332.9 3.9 fusion.52
  336.9 2.3 copy-done.6
  339.2 16.0 %fusion.96 = bf16[16,256,2048]{2,1,0:T(8,128)(2,1)} fusion(bf16[16,256,640]{2,1,0:T(8,128)(2,1)S(1)} %get-tuple-element.10, f32[640]{0:T(1024)S(1)} %copy-done.30, f32[16,256]{1,0:T(8,128)S(1)} %add_rsqrt_fusion.5, bf16[640,2048]{1,0:T(8,128)(2,1)S(1)} %copy-done), kind=kOutput, calls=%fused_computation.127 | convolution fusion | flops 10747904000 | bytes 24660480 | tf_op jit(solution)/shard_map/btd,df->btf/dot_general | solution.py:66
  355.2 34.3 %fusion.39 = (f32[16,256]{1,0:T(8,128)S(1)}, bf16[16,256,640]{2,1,0:T(8,128)(2,1)}) fusion(bf16[2048,640]{1,0:T(8,128)(2,1)} %param.32, bf16[16,256,2048]{2,1,0:T(8,128)(2,1)} %fusion.96, bf16[16,256,640]{2,1,0:T(8,128)(2,1)} %copy-done.6, f32[640]{0:T(1024)S(1)} %copy-done.30, f32[16,256]{1,0:T(8,128)S(1)} %add_rsqrt_fusion.5, bf16[640,2048]{1,0:T(8,128)(2,1)} %param.31), kind=kOutput, calls=%fused_computation.75 | convolution fusion | flops 21604855808 | bytes 32541184 | tf_op jit(solution)/shard_map/btf,fd->btd/dot_general | solution.py:69
  389.5 6.3 fusion.56
  396.0 2.3 bitcast_convert_fusion
  398.3 8.6 %fusion.139 = (bf16[16,256,1,128]{1,3,0,2:T(8,128)(2,1)S(1)}, bf16[16,256,1,128]{1,3,0,2:T(8,128)(2,1)S(1)}) fusion(f32[16,256,1,256]{1,3,0,2:T(8,128)S(1)} %bitcast_convert_fusion, f32[128]{0:T(128)S(1)} %copy-done.21, f32[16,256]{1,0:T(8,128)S(1)} %copy-done.15), kind=kLoop, calls=%fused_computation.159 | loop fusion | flops 4718592 | bytes 6308352 | tf_op jit(solution)/shard_map/convert.4
  406.9 1.5 pad_maximum_fusion.1
  409.1 6.1 fusion.30
  415.3 6.0 fusion.146
  422.5 12.8 %convert_convert_fusion = f32[16,256,1024]{2,1,0:T(8,128)} fusion(bf16[16,256,640]{2,1,0:T(8,128)(2,1)} %copy-done.4, f32[640]{0:T(1024)S(1)} %copy-done.29, f32[16,256]{1,0:T(8,128)S(1)} %add_rsqrt_fusion.3, bf16[640,1024]{1,0:T(8,128)(2,1)S(1)} %copy-done.32), kind=kOutput, calls=%fused_computation.106 | convolution fusion | flops 5387583488 | bytes 23349760 | tf_op jit(solution)/shard_map/btd,dn->btn/dot_general | solution.py:40
  435.3 17.6 %copy.44 = f32[16,256,1024]{1,2,0:T(8,128)} copy(f32[16,256,1024]{2,1,0:T(8,128)} %convert_convert_fusion) | data formatting | bytes 33554432 | tf_op jit(solution)/shard_map/convert_element_type | solution.py:28
  452.8 11.0 %fusion.182 = (f32[16,256,4,128]{1,3,2,0:T(8,128)}, f32[16,256,4,128]{1,3,2,0:T(8,128)}) fusion(f32[16,256,4,256]{1,3,2,0:T(8,128)} %bitcast.149), kind=kLoop, calls=%fused_computation.216 | loop fusion | bytes 33554432 | tf_op jit(solution)/shard_map/slice | solution.py:30
  463.9 9.3 %copy.71 = f32[16,256,4,128]{3,1,2,0:T(8,128)} copy(f32[16,256,4,128]{1,3,2,0:T(8,128)} %get-tuple-element.15) | data formatting | bytes 16777216
  473.2 9.4 %copy.70 = f32[16,256,4,128]{3,1,2,0:T(8,128)} copy(f32[16,256,4,128]{1,3,2,0:T(8,128)} %get-tuple-element.16) | data formatting | bytes 16777216
  482.6 11.6 %multiply_subtract_fusion = (f32[16,256,4,128]{3,1,2,0:T(8,128)}, f32[16,256,4,128]{3,1,2,0:T(8,128)}) fusion(f32[16,256,4,128]{3,1,2,0:T(8,128)} %copy.71, f32[16,256,4,128]{3,1,2,0:T(8,128)} %copy.70, f32[16,256,128]{2,1,0:T(8,128)} %get-tuple-element.26, f32[16,256,128]{2,1,0:T(8,128)S(1)} %copy-done.7), kind=kLoop, calls=%fused_computation.105 | loop fusion | flops 12582912 | bytes 37748736 | tf_op jit(solution)/shard_map/sub | solution.py:31
  494.2 35.2 %fusion.2 = (f32[16,4,256]{2,1,0:T(4,128)S(1)}, f32[16,1024,256,4]{2,1,3,0:T(8,128)}) fusion(pred[16,256,1024]{1,2,0:T(8,128)(4,1)} %fusion.30, f32[16,256,4,128]{3,1,2,0:T(8,128)} %get-tuple-element.12, f32[16,256,4,128]{3,1,2,0:T(8,128)} %get-tuple-element.11, bf16[16,1024,1,256]{1,3,0,2:T(8,128)(2,1)} %all-gather.4.cloned.1.call-done), kind=kOutput, calls=%fused_computation.16 | convolution fusion | flops 8669609984 | bytes 96534528 | tf_op jit(solution)/shard_map/btkgd,bskd->bkgts/dot_general | solution.py:51
  529.4 23.7 %fusion = f32[16,4,256]{2,1,0:T(4,128)S(1)} fusion(f32[16,1024,256,4]{2,1,3,0:T(8,128)} %get-tuple-element.34, f32[16,4,256]{2,1,0:T(4,128)S(1)} %get-tuple-element.33, pred[16,256,1024]{1,2,0:T(8,128)(4,1)} %fusion.30), kind=kLoop, calls=%fused_computation.3 | loop fusion | flops 83869696 | bytes 71434240 | tf_op jit(solution)/shard_map/reduce_sum | solution.py:55
  553.1 35.0 %fusion.75 = bf16[16,256,4,256]{3,1,2,0:T(8,128)(2,1)} fusion(f32[16,4,256]{2,1,0:T(4,128)S(1)} %fusion, f32[16,4,256]{2,1,0:T(4,128)S(1)} %get-tuple-element.33, f32[16,1024,256,4]{2,1,3,0:T(8,128)} %get-tuple-element.34, pred[16,256,1024]{1,2,0:T(8,128)(4,1)} %fusion.30, bf16[16,1024,256]{1,2,0:T(8,128)(2,1)} %all-gather.6.cloned.1.call-done), kind=kOutput, calls=%fused_computation.113 | convolution fusion | flops 8694792192 | bytes 88211456 | tf_op jit(solution)/shard_map/bkgts,bskd->btkgd/dot_general | solution.py:56
  588.1 9.5 %fusion.42 = (f32[16,256]{1,0:T(8,128)S(1)}, bf16[16,256,640]{2,1,0:T(8,128)(2,1)S(1)}) fusion(bf16[16,256,1024]{1,2,0:T(8,128)(2,1)} %bitcast.153, bf16[1024,640]{1,0:T(8,128)(2,1)S(1)} %copy-done.33), kind=kOutput, calls=%fused_computation.78 | convolution fusion | flops 5379190784 | bytes 14958592 | tf_op jit(solution)/shard_map/btn,nd->btd/dot_general | solution.py:63
  597.6 3.9 fusion.60
  601.6 2.3 copy-done.2
  603.9 17.9 %fusion.92 = bf16[16,256,2048]{2,1,0:T(8,128)(2,1)} fusion(bf16[16,256,640]{2,1,0:T(8,128)(2,1)S(1)} %get-tuple-element.6, f32[640]{0:T(1024)S(1)} %copy-done.31, f32[16,256]{1,0:T(8,128)S(1)} %add_rsqrt_fusion.1, bf16[640,2048]{1,0:T(8,128)(2,1)} %param.41), kind=kOutput, calls=%fused_computation.126 | convolution fusion | flops 10747904000 | bytes 24660480 | tf_op jit(solution)/shard_map/btd,df->btf/dot_general | solution.py:66
  621.8 34.0 %fusion.45 = (f32[16,256]{1,0:T(8,128)S(1)}, bf16[16,256,640]{2,1,0:T(8,128)(2,1)}) fusion(bf16[2048,640]{1,0:T(8,128)(2,1)} %param.43, bf16[16,256,2048]{2,1,0:T(8,128)(2,1)} %fusion.92, bf16[16,256,640]{2,1,0:T(8,128)(2,1)} %copy-done.2, f32[640]{0:T(1024)S(1)} %copy-done.31, f32[16,256]{1,0:T(8,128)S(1)} %add_rsqrt_fusion.1, bf16[640,2048]{1,0:T(8,128)(2,1)} %param.42), kind=kOutput, calls=%fused_computation.81 | convolution fusion | flops 21604855808 | bytes 32541184 | tf_op jit(solution)/shard_map/btf,fd->btd/dot_general | solution.py:69
  655.8 8.0 %fusion.63 = bf16[16,256,640]{2,1,0:T(8,128)(2,1)} fusion(bf16[16,256,640]{2,1,0:T(8,128)(2,1)} %copy-done.2, bf16[16,256,640]{2,1,0:T(8,128)(2,1)} %get-tuple-element.38, f32[640]{0:T(1024)S(1)} %copy-done.18, f32[16,256]{1,0:T(8,128)S(1)} %add_rsqrt_fusion), kind=kLoop, calls=%fused_computation.99 | loop fusion | flops 20971520 | bytes 15747584 | tf_op jit(solution)/shard_map/convert_element_type | solution.py:70
  (104 shorter events, 4.5 us)
Async XLA Ops:
  6.5 332.7 %copy-start = (bf16[640,2048]{1,0:T(8,128)(2,1)S(1)}, bf16[640,2048]{1,0:T(8,128)(2,1)}, u32[]{:S(2)}) copy-start(bf16[640,2048]{1,0:T(8,128)(2,1)} %param.30) | copy-start | bytes 7864324
  6.5 487.6 %all-gather.4.cloned.1.call-start = ((), (), s32[]{:S(2)}) async-start(), calls=%async_computation | async-start | bytes 10485760 | tf_op jit(solution)/shard_map/all_gather | solution.py:97
  6.6 161.9 %copy-start.20 = (f32[128]{0:T(128)}, f32[128]{0:T(128)S(1)}, u32[]{:S(2)}) copy-start(f32[128]{0:T(128)S(1)} %negate_power_fusion) | copy-start | bytes 1540
  11.0 19.3 %slice-start = ((s8[5242880]{0:T(1024)(128)(4,1)}), s8[4194304]{0:T(1024)(128)(4,1)S(1)}, s32[]{:S(2)}) async-start(s8[5242880]{0:T(1024)(128)(4,1)} %bitcast.150), calls=%async_computation.2 | async-start | bytes 8388608
  11.9 156.6 %copy-start.14 = (f32[16,256]{1,0:T(8,128)}, f32[16,256]{1,0:T(8,128)S(1)}, u32[]{:S(2)}) copy-start(f32[16,256]{1,0:T(8,128)S(1)} %convert_element_type.221) | copy-start | bytes 49156
  11.9 18.4 %slice-start.1 = ((s8[5242880]{0:T(1024)(128)(4,1)}), s8[1048576]{0:T(1024)(128)(4,1)S(1)}, s32[]{:S(2)}) async-start(s8[5242880]{0:T(1024)(128)(4,1)} %bitcast.150), calls=%async_computation.3 | async-start | bytes 2097152
  11.9 18.5 %copy-start.34 = (bf16[640,256]{1,0:T(8,128)(2,1)S(1)}, bf16[640,256]{1,0:T(8,128)(2,1)}, u32[]{:S(2)}) copy-start(bf16[640,256]{1,0:T(8,128)(2,1)} %param.28) | copy-start | bytes 983044
  25.1 1.0 copy-start.8
  25.1 2.5 copy-start.9
  26.1 10.1 %copy-start.12 = (s32[16,256]{1,0:T(8,128)S(1)}, s32[16,256]{1,0:T(8,128)}, u32[]{:S(2)}) copy-start(s32[16,256]{1,0:T(8,128)} %param.25) | copy-start | bytes 49156
  27.6 149.7 %copy-start.22 = (f32[640]{0:T(1024)S(1)}, f32[640]{0:T(1024)}, u32[]{:S(2)}) copy-start(f32[640]{0:T(1024)} %param.36) | copy-start | bytes 7684
  27.6 150.3 %copy-start.23 = (f32[640]{0:T(1024)S(1)}, f32[640]{0:T(1024)}, u32[]{:S(2)}) copy-start(f32[640]{0:T(1024)} %param.34) | copy-start | bytes 7684
  27.6 214.4 %collective-permute-start.3 = (bf16[16,256,1,256]{1,3,0,2:T(8,128)(2,1)}, bf16[16,256,1,256]{1,3,0,2:T(8,128)(2,1)}, u32[]{:S(2)}, u32[]{:S(2)}) collective-permute-start(bf16[16,256,1,256]{1,3,0,2:T(8,128)(2,1)} %pad_maximum_fusion), channel_id=1, source_target_pairs={{0,2},{1,3},{4,6},{5,7}} | collective-permute-start | bytes 6291464 | tf_op jit(solution)/shard_map/ppermute | solution.py:90
  29.0 212.9 %collective-permute-start.2 = (bf16[16,256,1,256]{1,3,0,2:T(8,128)(2,1)}, bf16[16,256,1,256]{1,3,0,2:T(8,128)(2,1)}, u32[]{:S(2)}, u32[]{:S(2)}) collective-permute-start(bf16[16,256,1,256]{1,3,0,2:T(8,128)(2,1)} %pad_maximum_fusion), channel_id=1, source_target_pairs={{0,1},{1,2},{2,3},{4,5},{5,6},{6,7}} | collective-permute-start | bytes 6291464 | tf_op jit(solution)/shard_map/ppermute | solution.py:90
  33.6 261.7 %collective-permute-start.1 = (bf16[16,256,1,256]{3,1,0,2:T(8,128)(2,1)}, bf16[16,256,1,256]{3,1,0,2:T(8,128)(2,1)}, u32[]{:S(2)}, u32[]{:S(2)}) collective-permute-start(bf16[16,256,1,256]{3,1,0,2:T(8,128)(2,1)} %convert_bitcast_fusion), channel_id=1, source_target_pairs={{0,2},{1,3},{4,6},{5,7}} | collective-permute-start | bytes 6291464 | tf_op jit(solution)/shard_map/ppermute | solution.py:91
  34.9 260.5 %collective-permute-start = (bf16[16,256,1,256]{3,1,0,2:T(8,128)(2,1)}, bf16[16,256,1,256]{3,1,0,2:T(8,128)(2,1)}, u32[]{:S(2)}, u32[]{:S(2)}) collective-permute-start(bf16[16,256,1,256]{3,1,0,2:T(8,128)(2,1)} %convert_bitcast_fusion), channel_id=1, source_target_pairs={{0,1},{1,2},{2,3},{4,5},{5,6},{6,7}} | collective-permute-start | bytes 6291464 | tf_op jit(solution)/shard_map/ppermute | solution.py:91
  168.4 56.0 %copy-start.10 = (s32[16,1024]{1,0:T(8,128)}, s32[16,1024]{1,0:T(8,128)S(1)}, u32[]{:S(2)}) copy-start(s32[16,1024]{1,0:T(8,128)S(1)} %all_gather.9) | copy-start | bytes 196612
  211.8 11.4 %copy-start.24 = (f32[640]{0:T(1024)S(1)}, f32[640]{0:T(1024)}, u32[]{:S(2)}) copy-start(f32[640]{0:T(1024)} %param.35) | copy-start | bytes 7684
  211.8 12.0 %copy-start.25 = (f32[640]{0:T(1024)S(1)}, f32[640]{0:T(1024)}, u32[]{:S(2)}) copy-start(f32[640]{0:T(1024)} %param.44) | copy-start | bytes 7684
  322.8 10.1 %copy-start.3 = (bf16[16,256,640]{2,1,0:T(8,128)(2,1)S(1)}, bf16[16,256,640]{2,1,0:T(8,128)(2,1)}, u32[]{:S(2)}) copy-start(bf16[16,256,640]{2,1,0:T(8,128)(2,1)} %param.24) | copy-start | bytes 15728644
  322.8 10.1 %copy-start.17 = (f32[640]{0:T(1024)S(1)}, f32[640]{0:T(1024)}, u32[]{:S(2)}) copy-start(f32[640]{0:T(1024)} %broadcast_add_fusion.6) | copy-start | bytes 7684
  332.9 6.3 copy-start.30
  336.9 2.4 copy-start.6
  355.2 34.3 %copy-start.16 = (f32[640]{0:T(1024)S(1)}, f32[640]{0:T(1024)}, u32[]{:S(2)}) copy-start(f32[640]{0:T(1024)} %broadcast_add_fusion.4) | copy-start | bytes 7684
  389.5 6.4 copy-start.29
  389.5 6.4 copy-start.35
  395.9 11.0 %copy-start.4 = (bf16[16,256,640]{2,1,0:T(8,128)(2,1)}, bf16[16,256,640]{2,1,0:T(8,128)(2,1)S(1)}, u32[]{:S(2)}) copy-start(bf16[16,256,640]{2,1,0:T(8,128)(2,1)S(1)} %get-tuple-element.8) | copy-start | bytes 15728644
  395.9 2.4 copy-start.15
  395.9 2.4 copy-start.21
  398.3 10.2 %copy-start.26 = (f32[640]{0:T(1024)S(1)}, f32[640]{0:T(1024)}, u32[]{:S(2)}) copy-start(f32[640]{0:T(1024)} %param.45) | copy-start | bytes 7684
  398.3 10.8 %copy-start.11 = (s32[16,1024]{1,0:T(8,128)S(1)}, s32[16,1024]{1,0:T(8,128)}, u32[]{:S(2)}) copy-start(s32[16,1024]{1,0:T(8,128)} %copy-done.10) | copy-start | bytes 196612
  398.3 10.8 %copy-start.13 = (s32[16,256]{1,0:T(8,128)S(1)}, s32[16,256]{1,0:T(8,128)}, u32[]{:S(2)}) copy-start(s32[16,256]{1,0:T(8,128)} %param.25) | copy-start | bytes 49156
  398.3 17.0 %copy-start.36 = (bf16[640,256]{1,0:T(8,128)(2,1)S(1)}, bf16[640,256]{1,0:T(8,128)(2,1)}, u32[]{:S(2)}) copy-start(bf16[640,256]{1,0:T(8,128)(2,1)} %param.39) | copy-start | bytes 983044
  408.5 144.6 %all-gather.6.cloned.1.call-start = ((), (), s32[]{:S(2)}) async-start(), calls=%async_computation.1 | async-start | bytes 10485760 | tf_op jit(solution)/shard_map/all_gather | solution.py:98
  409.1 12.2 %copy-start.27 = (f32[640]{0:T(1024)S(1)}, f32[640]{0:T(1024)}, u32[]{:S(2)}) copy-start(f32[640]{0:T(1024)} %param.46) | copy-start | bytes 7684
  409.1 12.8 %copy-start.28 = (f32[640]{0:T(1024)S(1)}, f32[640]{0:T(1024)}, u32[]{:S(2)}) copy-start(f32[640]{0:T(1024)} %param.47) | copy-start | bytes 7684
  409.1 13.3 %copy-start.32 = (bf16[640,1024]{1,0:T(8,128)(2,1)S(1)}, bf16[640,1024]{1,0:T(8,128)(2,1)}, u32[]{:S(2)}) copy-start(bf16[640,1024]{1,0:T(8,128)(2,1)} %param.37) | copy-start | bytes 3932164
  473.2 9.4 %copy-start.7 = (f32[16,256,128]{2,1,0:T(8,128)S(1)}, f32[16,256,128]{2,1,0:T(8,128)}, u32[]{:S(2)}) copy-start(f32[16,256,128]{2,1,0:T(8,128)} %get-tuple-element.25) | copy-start | bytes 6291460
  553.1 35.0 %copy-start.33 = (bf16[1024,640]{1,0:T(8,128)(2,1)S(1)}, bf16[1024,640]{1,0:T(8,128)(2,1)}, u32[]{:S(2)}) copy-start(bf16[1024,640]{1,0:T(8,128)(2,1)} %param.40) | copy-start | bytes 3932164
  588.1 9.5 %copy-start.5 = (bf16[16,256,640]{2,1,0:T(8,128)(2,1)S(1)}, bf16[16,256,640]{2,1,0:T(8,128)(2,1)}, u32[]{:S(2)}) copy-start(bf16[16,256,640]{2,1,0:T(8,128)(2,1)} %copy-done.4) | copy-start | bytes 15728644
  588.1 9.5 %copy-start.19 = (f32[640]{0:T(1024)S(1)}, f32[640]{0:T(1024)}, u32[]{:S(2)}) copy-start(f32[640]{0:T(1024)} %broadcast_add_fusion.2) | copy-start | bytes 7684
  597.6 6.3 copy-start.31
  601.6 2.4 copy-start.2
  621.8 34.0 %copy-start.18 = (f32[640]{0:T(1024)S(1)}, f32[640]{0:T(1024)}, u32[]{:S(2)}) copy-start(f32[640]{0:T(1024)} %broadcast_add_fusion) | copy-start | bytes 7684
  621.8 42.0 %copy-start.1 = (bf16[640,2048]{1,0:T(8,128)(2,1)S(1)}, bf16[640,2048]{1,0:T(8,128)(2,1)}, u32[]{:S(2)}) copy-start(bf16[640,2048]{1,0:T(8,128)(2,1)} %param.30) | copy-start | bytes 7864324
Sparse Core Ops, SparseCore 0:
  408.6 57.1 all-gather.3
  467.3 56.8 all-gather.5
where the time goes:
time: 679 us; the launch traced here: 671 us
  matrix products  291 us (43%)
  other arithmetic  144 us (21%)
  blocking collectives  132 us (19%)
  local copies, waits for them, and re-layouts  84.9 us (13%)
  between operations  14.1 us (2%)
    all_gather x1, blocking collectives, device_step(): all_pos = lax.all_gather(positions, 'cp', axis=1, tiled=True)  132 us
    dot_general x2, matrix products, finish_layer(): jnp.einsum('btf,fd->btd', act_val, w_down, preferred_element_type=jnp.flo...  68.3 us
    dot_general x2, matrix products, attend(): jnp.einsum('btkgd,bskd->bkgts', query_rot, key_all, preferred_element_typ...  64.5 us
    dot_general x2, matrix products, attend(): jnp.einsum('bkgts,bskd->btkgd', prob_bf, value_all, preferred_element_typ...  62.4 us
    reduce_sum x2, other arithmetic, attend(): jax.nn.softmax(jnp.where(visible, capped, -1e+30), axis=-1)  47.7 us
    convert_element_type x2, local copies, waits for them, and re-layouts, apply_rope(): widened = heads_in.astype(jnp.float32)  38 us
    dot_general x2, matrix products, finish_layer(): jnp.einsum('btd,df->btf', normed_mid, w_gate, preferred_element_type=jnp....  33.9 us
    dot_general x2, matrix products, project_qkv(): jnp.einsum('btd,dn->btn', normed, w_q, preferred_element_type=jnp.float32)  25.8 us
  transfers between devices with their start and end apart: 6, of which 0 were waited for; matrix products, arithmetic and copies ran while one was open for 41% of the time, Pallas kernels for 0%

commit v1 on v0

v1 whole, which is shorter than its diff:
```python
import functools

import jax
import jax.numpy as jnp
import numpy as np
from jax import lax
from jax.experimental import pallas as pl
from jax.experimental.pallas import tpu as pltpu
from jax.sharding import PartitionSpec as P

DIM = 640
HEADS = 4
HD = 256
HALF = HD // 2
FFN = 2048
WINDOW = 512
EPSILON = 1e-6
THETA = 10000.0
SOFT_CAP = 50.0
LOG2E = 1.4426950408889634
BLK = 256
NCP = 4
ROWS = 4
QKV = HEADS * HD + 2 * HD
FCH = 512
LOW = 64
HIGH = 32
BF = jnp.bfloat16
F32 = jnp.float32


def rope_lookup():
    inv_freq = THETA ** (-(np.arange(HALF, dtype=np.float64) * 2.0 / HD))
    table = np.zeros((128, 4 * HALF), np.float64)
    high = np.arange(HIGH)[:, None] * float(LOW) * inv_freq
    low = np.arange(LOW)[:, None] * inv_freq
    table[:HIGH, 0:HALF] = np.cos(high)
    table[:HIGH, HALF : 2 * HALF] = np.sin(high)
    table[HIGH : HIGH + LOW, 2 * HALF : 3 * HALF] = np.cos(low)
    table[HIGH : HIGH + LOW, 3 * HALF :] = np.sin(low)
    parts = []
    rest = table
    for _ in range(3):
        part = rest.astype(jnp.bfloat16)
        parts.append(part)
        rest = rest - part.astype(np.float64)
    return np.concatenate(parts, axis=1)


def dot(lhs, rhs):
    return jnp.dot(lhs, rhs, preferred_element_type=F32)


def rms(wide, gain):
    mean_sq = jnp.mean(wide * wide, axis=-1, keepdims=True)
    return (wide * lax.rsqrt(mean_sq + EPSILON) * gain).astype(BF)


def kernel(
    hid, pos, gains, table, *rest
):
    weights = rest[:14]
    out = rest[14]
    (x_buf, pos_buf, w_qkv, w_o, w_gu, w_d, k_buf, v_buf, q_buf, o_buf, e_buf, h_buf, cos_buf, sin_buf, qp_buf,
     w_sem, in_send, in_recv, pos_send, pos_recv, out_send, out_recv) = rest[15:]
    me = lax.axis_index("cp")

    def weight_copies(layer):
        w_q, w_k, w_v, wo, wg, wu, wd = weights[7 * layer : 7 * layer + 7]
        places = (
            (w_q, w_qkv.at[layer, :, 0:1024]),
            (w_k, w_qkv.at[layer, :, 1024:1280]),
            (w_v, w_qkv.at[layer, :, 1280:1536]),
            (wo, w_o.at[layer]),
            (wg, w_gu.at[layer, :, 0:FFN]),
            (wu, w_gu.at[layer, :, FFN : 2 * FFN]),
            (wd, w_d.at[layer]),
        )
        return [pltpu.make_async_copy(src, dst, w_sem.at[layer, i]) for i, (src, dst) in enumerate(places)]

    def peer(shift):
        return lax.rem(me + shift, NCP)

    def send_piece(row, dest):
        return pltpu.make_async_remote_copy(
            src_ref=hid.at[dest * ROWS + row],
            dst_ref=x_buf.at[row, me],
            send_sem=in_send.at[row, dest],
            recv_sem=in_recv.at[row, me],
            device_id={"cp": dest},
            device_id_type=pl.DeviceIdType.MESH,
        )

    def own_piece(row):
        return pltpu.make_async_copy(hid.at[me * ROWS + row], x_buf.at[row, me], in_recv.at[row, me])

    def send_pos(dest):
        return pltpu.make_async_remote_copy(
            src_ref=pos.at[dest],
            dst_ref=pos_buf.at[me],
            send_sem=pos_send.at[dest],
            recv_sem=pos_recv.at[me],
            device_id={"cp": dest},
            device_id_type=pl.DeviceIdType.MESH,
        )

    def own_pos():
        return pltpu.make_async_copy(pos.at[me], pos_buf.at[me], pos_recv.at[me])

    def send_out(row, piece):
        return pltpu.make_async_remote_copy(
            src_ref=x_buf.at[row, piece],
            dst_ref=out.at[me * ROWS + row],
            send_sem=out_send.at[row, piece],
            recv_sem=out_recv.at[me * ROWS + row],
            device_id={"cp": piece},
            device_id_type=pl.DeviceIdType.MESH,
        )

    def own_out(row):
        return pltpu.make_async_copy(x_buf.at[row, me], out.at[me * ROWS + row], out_send.at[row, me])

    for copy in weight_copies(0)[:3]:
        copy.start()
    own_piece(0).start()
    own_pos().start()

    barrier = pltpu.get_barrier_semaphore()
    for shift in range(1, NCP):
        pl.semaphore_signal(barrier, inc=1, device_id={"cp": peer(shift)}, device_id_type=pl.DeviceIdType.MESH)
    pl.semaphore_wait(barrier, NCP - 1)

    core = lax.rem(me, 2)
    partner = me + 1 - 2 * core
    far_0 = lax.rem(me + 2 - core, NCP)
    far_1 = lax.rem(me + 3 - core, NCP)
    for shift in range(1, NCP):
        send_pos(peer(shift)).start()
    send_piece(0, partner).start()

    @pl.when(core == 0)
    def _():
        send_piece(0, far_0).start()
        send_piece(0, far_1).start()

    for copy in weight_copies(0)[3:] + weight_copies(1):
        copy.start()
    for row in range(1, ROWS):
        own_piece(row).start()
    own_pos().wait()
    for shift in range(1, NCP):
        src = peer(shift)
        pltpu.make_async_copy(pos_buf.at[src], pos_buf.at[src], pos_recv.at[src]).wait()

    def attention(layer, first, count, row):
        keys = count * BLK
        base = pl.multiple_of(first * BLK, BLK) if not isinstance(first, int) else first * BLK
        below = lax.broadcasted_iota(jnp.int32, (BLK, BLK), 0) >= lax.broadcasted_iota(jnp.int32, (BLK, BLK), 1)
        q_low = qp_buf[...] - float(WINDOW)
        for head in range(HEADS):
            query = q_buf[head]
            total = jnp.zeros((BLK, 128), F32)
            for j in range(count):
                key = k_buf[layer, pl.ds(base + j * BLK, BLK), :]
                score = lax.dot_general(query, key, (((1,), (1,)), ((), ())), preferred_element_type=F32)
                soft = jnp.exp2(jnp.tanh(score * (1.0 / SOFT_CAP)) * (SOFT_CAP * LOG2E))
                if j == count - 1:
                    soft = jnp.where(below, soft, 0.0)
                elif layer == 0:
                    k_pos = pos_buf[first + j, pl.ds(row, 1), :].astype(F32)
                    halves = []
                    for lo in (0, 128):
                        halves.append(jnp.where(q_low < k_pos[:, lo : lo + 128], soft[:, lo : lo + 128], 0.0))
                    soft = jnp.concatenate(halves, axis=1)
                e_buf[head, :, j * BLK : (j + 1) * BLK] = soft
                total = total + (soft[:, :128] + soft[:, 128:])
            inverse = 1.0 / jnp.sum(total, axis=-1, keepdims=True)
            prob = (e_buf[head, :, 0:keys] * inverse).astype(BF)
            mixed = dot(prob, v_buf[layer, pl.ds(base, keys), :])
            o_buf[:, head * HD : (head + 1) * HD] = mixed.astype(BF)

    def step(it, carry):
        layer = lax.rem(it, 2)
        piece = lax.rem(it // 2, NCP)
        row = it // (2 * NCP)
        x_ref = x_buf.at[row, piece]

        @pl.when(layer == 0)
        def _():
            pltpu.make_async_copy(x_ref, x_ref, in_recv.at[row, piece]).wait()
            row_pos = pos_buf[piece, pl.ds(row, 1), :]
            col_pos = jnp.transpose(jnp.broadcast_to(row_pos.astype(F32), (128, BLK)))
            qp_buf[...] = col_pos
            whole = col_pos.astype(jnp.int32)
            lane = lax.broadcasted_iota(jnp.int32, (BLK, 128), 1)
            hit = (lane == (whole >> 6)) | (lane == (whole & (LOW - 1)) + HIGH)
            found = dot(jnp.where(hit, 1.0, 0.0).astype(BF), table[...])
            width = 4 * HALF
            found = found[:, :width] + found[:, width : 2 * width] + found[:, 2 * width :]
            c_hi, s_hi = found[:, 0:HALF], found[:, HALF : 2 * HALF]
            c_lo, s_lo = found[:, 2 * HALF : 3 * HALF], found[:, 3 * HALF :]
            cos_buf[...] = c_hi * c_lo - s_hi * s_lo
            sin_buf[...] = s_hi * c_lo + c_hi * s_lo

        for first in range(2):
            @pl.when(it == first)
            def _():
                for copy in weight_copies(first)[:3]:
                    copy.wait()

        @pl.when((it == 1) & (core == 1))
        def _():
            send_piece(0, far_0).start()
            send_piece(0, far_1).start()

        @pl.when((piece == 1) & (layer == 0) & (row < ROWS - 1))
        def _():
            for dest in (partner, far_0, far_1):
                send_piece(row + 1, dest).start()

        normed = rms(x_ref[...].astype(F32), gains[pl.ds(layer * 4, 1), :])
        cos_t, sin_t = cos_buf[...], sin_buf[...]
        spot = pl.multiple_of(piece * BLK, BLK)

        def rotate(raw):
            wide = raw.astype(BF).astype(F32)
            one, two = wide[:, :HALF], wide[:, HALF:]
            return one * cos_t - two * sin_t, two * cos_t + one * sin_t

        for head in range(HEADS):
            one, two = rotate(dot(normed, w_qkv[layer, :, head * HD : (head + 1) * HD]))
            q_buf[head, :, :HALF] = (one * HD**-0.5).astype(BF)
            q_buf[head, :, HALF:] = (two * HD**-0.5).astype(BF)
        one, two = rotate(dot(normed, w_qkv[layer, :, 1024:1280]))
        k_buf[layer, pl.ds(spot, BLK), :HALF] = one.astype(BF)
        k_buf[layer, pl.ds(spot, BLK), HALF:] = two.astype(BF)
        v_buf[layer, pl.ds(spot, BLK), :] = dot(normed, w_qkv[layer, :, 1280:1536]).astype(BF)

        for count in range(1, 4):
            @pl.when((layer == 0) & (jnp.minimum(piece, 2) == count - 1))
            def _():
                attention(0, piece - (count - 1), count, row)
        for count in range(1, 5):
            @pl.when((layer == 1) & (piece == count - 1))
            def _():
                attention(1, 0, count, row)

        for first in range(2):
            @pl.when(it == first)
            def _():
                for copy in weight_copies(first)[3:]:
                    copy.wait()

        attn = dot(o_buf[...], w_o[layer]).astype(BF)
        delta = rms(attn.astype(F32), gains[pl.ds(layer * 4 + 1, 1), :])
        mid = (x_ref[...].astype(F32) + delta.astype(F32)).astype(BF)
        x_ref[...] = mid
        normed_mid = rms(mid.astype(F32), gains[pl.ds(layer * 4 + 2, 1), :])
        for lo in range(0, FFN, FCH):
            gate = dot(normed_mid, w_gu[layer, :, lo : lo + FCH]).astype(BF).astype(F32)
            up = dot(normed_mid, w_gu[layer, :, FFN + lo : FFN + lo + FCH]).astype(BF).astype(F32)
            inner = gate * (0.7978845608028654 + (0.7978845608028654 * 0.044715) * (gate * gate))
            h_buf[:, lo : lo + FCH] = ((0.5 * gate) * (1.0 + jnp.tanh(inner)) * up).astype(BF)
        down = dot(h_buf[...], w_d[layer]).astype(BF)
        delta = rms(down.astype(F32), gains[pl.ds(layer * 4 + 3, 1), :])
        x_ref[...] = (x_ref[...].astype(F32) + delta.astype(F32)).astype(BF)

        @pl.when((layer == 1) & (piece == me))
        def _():
            own_out(row).start()

        @pl.when((layer == 1) & (piece != me))
        def _():
            send_out(row, piece).start()

        return carry

    lax.fori_loop(0, ROWS * NCP * 2, step, 0)

    for shift in range(1, NCP):
        other = peer(shift)
        send_pos(other).wait_send()
        for row in range(ROWS):
            send_piece(row, other).wait_send()
            send_out(row, other).wait_send()
            place = out.at[other * ROWS + row]
            pltpu.make_async_copy(place, place, out_recv.at[other * ROWS + row]).wait()
    for row in range(ROWS):
        own_out(row).wait()


def device_step(hidden, positions, *params):
    local_w, global_w = params[:11], params[11:]
    gains = 1.0 + jnp.stack([*local_w[7:], *global_w[7:]])
    table = jnp.asarray(rope_lookup())
    pos = positions.reshape(NCP, ROWS, BLK)
    hbm = pl.BlockSpec(memory_space=pl.ANY)
    vmem = pl.BlockSpec(memory_space=pltpu.VMEM)
    dma = pltpu.SemaphoreType.DMA
    return pl.pallas_call(
        kernel,
        out_shape=jax.ShapeDtypeStruct(hidden.shape, hidden.dtype),
        in_specs=[hbm, hbm, vmem, vmem] + [hbm] * 14,
        out_specs=hbm,
        scratch_shapes=[
            pltpu.VMEM((ROWS, NCP, BLK, DIM), BF),
            pltpu.VMEM((NCP, ROWS, BLK), jnp.int32),
            pltpu.VMEM((2, DIM, QKV), BF),
            pltpu.VMEM((2, HEADS * HD, DIM), BF),
            pltpu.VMEM((2, DIM, 2 * FFN), BF),
            pltpu.VMEM((2, FFN, DIM), BF),
            pltpu.VMEM((2, NCP * BLK, HD), BF),
            pltpu.VMEM((2, NCP * BLK, HD), BF),
            pltpu.VMEM((HEADS, BLK, HD), BF),
            pltpu.VMEM((BLK, HEADS * HD), BF),
            pltpu.VMEM((HEADS, BLK, NCP * BLK), F32),
            pltpu.VMEM((BLK, FFN), BF),
            pltpu.VMEM((BLK, HALF), F32),
            pltpu.VMEM((BLK, HALF), F32),
            pltpu.VMEM((BLK, 128), F32),
            dma((2, 7)),
            dma((ROWS, NCP)),
            dma((ROWS, NCP)),
            dma((NCP,)),
            dma((NCP,)),
            dma((ROWS, NCP)),
            dma((NCP * ROWS,)),
        ],
        compiler_params=pltpu.CompilerParams(
            collective_id=0, has_side_effects=True, vmem_limit_bytes=60 * 1024 * 1024
        ),
        name="layers",
    )(hidden, pos, gains, table, *local_w[:7], *global_w[:7])


def solution(mesh):
    specs_in = tuple([P("dp", "cp"), P("dp", "cp")] + [P()] * 22)
    return jax.shard_map(device_step, mesh=mesh, in_specs=specs_in, out_specs=P("dp", "cp"), check_vma=False)
```

time: 679 us -> 227 us (0.33); the launches traced: 671 us -> 226 us
  matrix products: 291 us -> 0 us
  Pallas kernels: 0 us -> 213 us
  other arithmetic: 144 us -> 0.61 us
  blocking collectives: 132 us -> 0 us
  local copies, waits for them, and re-layouts: 84.9 us -> 12.4 us
  between operations: 14.1 us -> 0.01 us
    dot_general x16 -> x0, matrix products: 291 us -> none  [the longest x2 68.3 us: finish_layer(): jnp.einsum('btf,fd->btd', act_val, w_down, preferred_element_type=jnp.flo...]
    pallas_call x0 -> x1, Pallas kernels: none -> 213 us  [device_step(): pl.pallas_call(kernel, out_shape=jax.ShapeDtypeStruct(hidden.shape, hidde...]
    all_gather x1 -> x0, blocking collectives: 132 us -> none  [device_step(): all_pos = lax.all_gather(positions, 'cp', axis=1, tiled=True)]
    reduce_sum x6 -> x0, other arithmetic: 65.5 us -> none  [the longest x2 47.7 us: attend(): jax.nn.softmax(jnp.where(visible, capped, -1e+30), axis=-1)]
    convert_element_type x2 -> x0, local copies, waits for them, and re-layouts: 38 us -> none  [apply_rope(): widened = heads_in.astype(jnp.float32)]
    sub x2 -> x0, other arithmetic: 23.9 us -> none  [apply_rope(): first_half * cos_t - second_half * sin_t]
    slice x2 -> x0, local copies, waits for them, and re-layouts: 22.4 us -> none  [the longest x1 11.4 us: apply_rope(): first_half = widened[..., :half_dim]]
    unnamed x80 -> x1, local copies, waits for them, and re-layouts: 24.5 us -> 5.52 us
  transfers between devices with their start and end apart: 6 -> 0, of which waited for: 0 -> 0; matrix products, arithmetic and copies ran while one was open for 41% -> 0% of each run, Pallas kernels for 0% -> 0%
where the time goes in v1:
time: 227 us; the launch traced here: 226 us
  Pallas kernels  213 us (94%)
  local copies, waits for them, and re-layouts  12.4 us (5%)
    pallas_call x1, Pallas kernels, device_step(): pl.pallas_call(kernel, out_shape=jax.ShapeDtypeStruct(hidden.shape, hidde...  213 us
    another operation x9, local copies, waits for them, and re-layouts, device_step(): gains = 1.0 + jnp.stack([*local_w[7:], *global_w[7:]])  5.55 us
    unnamed x1, local copies, waits for them, and re-layouts  5.52 us

profile of v1, /device:TPU:3, one launch (start us, length us, event | category | flops | bytes accessed | tf_op | source)
XLA Modules:
  0.0 225.7 jit_solution(8039137432599181607)
XLA Ops:
  0.0 0.7 stack.27
  0.7 0.7 stack.28
  1.4 0.7 stack.29
  2.1 0.7 stack.30
  2.8 0.7 stack.31
  3.4 0.7 stack.32
  4.1 0.7 stack.33
  4.8 0.7 stack.34
  5.6 0.6 broadcast_add_fusion.gains
  6.2 1.3 reshape.3.pos
  7.5 212.7 %layers.1 = bf16[16,256,640]{2,1,0:T(8,128)(2,1)} custom-call(bf16[16,256,640]{2,1,0:T(8,128)(2,1)} %hid.1, s32[4,4,256]{2,1,0:T(4,128)} %reshape.3.pos, f32[8,640]{1,0:T(8,128)} %broadcast_add_fusion.gains, bf16[128,1536]{1,0:T(8,128)(2,1)} %constant.4.clone.table, bf16[640,1024]{1,0:T(8,128)(2,1)} %rest_0_.1, bf16[640,256]{1,0:T(8,128)(2,1)} %rest_1_.1, ...), custom_call_target="tpu_custom_call" | custom-call | tf_op jit(solution)/shard_map/layers/pallas_call | solution.py:300
  220.2 5.5 %copy.27 = bf16[16,256,640]{2,1,0:T(8,128)(2,1)} copy(bf16[16,256,640]{2,1,0:T(8,128)(2,1)} %layers.1) | data formatting | bytes 10485760
  (1 shorter events, 0.0 us)

commit v2 on v1

v2 whole, which is shorter than its diff:
```python
import functools

import jax
import jax.numpy as jnp
import numpy as np
from jax import lax
from jax.experimental import pallas as pl
from jax.experimental.pallas import tpu as pltpu
from jax.sharding import PartitionSpec as P

DIM = 640
HEADS = 4
HD = 256
HALF = HD // 2
FFN = 2048
WINDOW = 512
EPSILON = 1e-6
THETA = 10000.0
SOFT_CAP = 50.0
LOG2E = 1.4426950408889634
BLK = 256
NCP = 4
ROWS = 4
UNITS = ROWS * NCP * 2
QKV = HEADS * HD + 2 * HD
FCH = 256
NROW = 64
NCH = {0: 256, 256: 256, 512: 128}
LOW = 64
HIGH = 32
BF = jnp.bfloat16
F32 = jnp.float32
MESH = pl.DeviceIdType.MESH


def rope_lookup():
    inv_freq = THETA ** (-(np.arange(HALF, dtype=np.float64) * 2.0 / HD))
    table = np.zeros((128, 4 * HALF), np.float64)
    high = np.arange(HIGH)[:, None] * float(LOW) * inv_freq
    low = np.arange(LOW)[:, None] * inv_freq
    table[:HIGH, 0:HALF] = np.cos(high)
    table[:HIGH, HALF : 2 * HALF] = np.sin(high)
    table[HIGH : HIGH + LOW, 2 * HALF : 3 * HALF] = np.cos(low)
    table[HIGH : HIGH + LOW, 3 * HALF :] = np.sin(low)
    parts = []
    rest = table
    for _ in range(3):
        part = rest.astype(jnp.bfloat16)
        parts.append(part)
        rest = rest - part.astype(np.float64)
    return np.concatenate(parts, axis=0)


def dot(lhs, rhs):
    return jnp.dot(lhs, rhs, preferred_element_type=F32)


def rms(wide, gain):
    mean_sq = jnp.mean(wide * wide, axis=-1, keepdims=True)
    tall = (wide * lax.rsqrt(mean_sq + EPSILON)).reshape(-1, 8, DIM) * gain[None]
    return tall.reshape(-1, DIM).astype(BF)


def unit(k):
    stream = lax.rem(k, 2)
    turn = k // 2
    layer = lax.rem(turn, 2)
    piece = lax.rem(turn // 2, NCP)
    row = (turn // (2 * NCP)) * 2 + stream
    return stream, layer, piece, row


def kernel(hid, pos, table, *rest):
    scales = rest[:8]
    weights = rest[8:22]
    out = rest[22]
    (x_buf, pos_buf, w_qkv, w_o, w_gu, w_d, k_buf, v_buf, q_buf, o_buf, e_buf, h_buf, a_buf, m_buf, t_buf, d_buf, mid_buf, cos_buf,
     sin_buf, qp_buf, gains, w_sem, in_send, in_recv, pos_send, pos_recv, out_send, out_recv) = rest[23:]
    me = lax.axis_index("cp")

    def weight_copies(layer):
        w_q, w_k, w_v, wo, wg, wu, wd = weights[7 * layer : 7 * layer + 7]
        places = (
            (w_q, w_qkv.at[layer, :, 0:1024]),
            (w_k, w_qkv.at[layer, :, 1024:1280]),
            (w_v, w_qkv.at[layer, :, 1280:1536]),
            (wo, w_o.at[layer]),
            (wg, w_gu.at[layer, :, 0:FFN]),
            (wu, w_gu.at[layer, :, FFN : 2 * FFN]),
            (wd, w_d.at[layer]),
        )
        return [pltpu.make_async_copy(src, dst, w_sem.at[layer, i]) for i, (src, dst) in enumerate(places)]

    def peer(shift):
        return lax.rem(me + shift, NCP)

    def send_piece(row, dest):
        return pltpu.make_async_remote_copy(
            src_ref=hid.at[dest * ROWS + row],
            dst_ref=x_buf.at[row * NCP + me],
            send_sem=in_send.at[row, dest],
            recv_sem=in_recv.at[row * NCP + me],
            device_id={"cp": dest},
            device_id_type=MESH,
        )

    def own_piece(row):
        return pltpu.make_async_copy(hid.at[me * ROWS + row], x_buf.at[row * NCP + me], in_recv.at[row * NCP + me])

    def send_pos(dest):
        return pltpu.make_async_remote_copy(
            src_ref=pos,
            dst_ref=pos_buf.at[me],
            send_sem=pos_send.at[dest],
            recv_sem=pos_recv.at[me],
            device_id={"cp": dest},
            device_id_type=MESH,
        )

    def own_pos():
        return pltpu.make_async_copy(pos, pos_buf.at[me], pos_recv.at[me])

    def send_out(row, piece):
        return pltpu.make_async_remote_copy(
            src_ref=x_buf.at[row * NCP + piece],
            dst_ref=out.at[me * ROWS + row],
            send_sem=out_send.at[row, piece],
            recv_sem=out_recv.at[me * ROWS + row],
            device_id={"cp": piece},
            device_id_type=MESH,
        )

    def own_out(row):
        return pltpu.make_async_copy(x_buf.at[row * NCP + me], out.at[me * ROWS + row], out_send.at[row, me])

    for copy in weight_copies(0)[:3]:
        copy.start()
    own_piece(0).start()
    own_pos().start()
    own_piece(1).start()

    barrier = pltpu.get_barrier_semaphore()
    for shift in range(1, NCP):
        pl.semaphore_signal(barrier, inc=1, device_id={"cp": peer(shift)}, device_id_type=MESH)
    pl.semaphore_wait(barrier, NCP - 1)

    core = lax.rem(me, 2)
    partner = me + 1 - 2 * core
    far_0 = lax.rem(me + 2 - core, NCP)
    far_1 = lax.rem(me + 3 - core, NCP)
    for shift in range(1, NCP):
        send_pos(peer(shift)).start()
    for row in range(2):
        send_piece(row, partner).start()

    @pl.when(core == 0)
    def _():
        for row in range(2):
            send_piece(row, far_0).start()
            send_piece(row, far_1).start()

    for copy in weight_copies(0)[3:] + weight_copies(1):
        copy.start()
    for row in range(2, ROWS):
        own_piece(row).start()
    for i in range(8):
        gains[i] = jnp.broadcast_to(1.0 + scales[i][...].reshape(1, DIM), (8, DIM))
    own_pos().wait()
    for shift in range(1, NCP):
        src = peer(shift)
        pltpu.make_async_copy(pos_buf.at[src], pos_buf.at[src], pos_recv.at[src]).wait()

    def positions_of(piece, row):
        return pos_buf[piece, pl.ds(me * ROWS + row, 1), :].astype(F32)

    def receive(k):
        _, _, piece, row = unit(k)
        x_ref = x_buf.at[row * NCP + piece]
        pltpu.make_async_copy(x_ref, x_ref, in_recv.at[row * NCP + piece]).wait()

    def rope(stream, index, half):
        piece = lax.rem(index, NCP)
        row = jnp.minimum(index // NCP, 1) * 2 + stream
        slot = stream * 2 + lax.rem(index, 2)
        spot = pl.multiple_of(half * 128, 128)
        whole_row = positions_of(piece, row)
        row_pos = jnp.where(half == 0, whole_row[:, :128], whole_row[:, 128:])
        col_pos = jnp.transpose(jnp.broadcast_to(row_pos, (128, 128)))
        whole = col_pos.astype(jnp.int32)
        lane = lax.broadcasted_iota(jnp.int32, (128, 128), 1)
        hit = jnp.where((lane == (whole >> 6)) | (lane == (whole & (LOW - 1)) + HIGH), 1.0, 0.0).astype(BF)
        found = dot(jnp.concatenate([hit, hit], axis=1), table[0:256, :]) + dot(hit, table[256:384, :])
        c_hi, s_hi = found[:, 0:HALF], found[:, HALF : 2 * HALF]
        c_lo, s_lo = found[:, 2 * HALF : 3 * HALF], found[:, 3 * HALF :]
        qp_buf[slot, pl.ds(spot, 128), :] = col_pos
        cos_buf[slot, pl.ds(spot, 128), :] = c_hi * c_lo - s_hi * s_lo
        sin_buf[slot, pl.ds(spot, 128), :] = s_hi * c_lo + c_hi * s_lo

    def enter(k):
        _, layer, piece, row = unit(k)
        for lo in range(0, BLK, NROW):
            part = x_buf[row * NCP + piece, lo : lo + NROW, :].astype(F32)
            a_buf[lo : lo + NROW, :] = rms(part, gains[layer * 4])

    def attend(k, count):
        stream, layer, piece, row = unit(k)
        turn = stream * 2 + lax.rem(piece, 2)
        cos_t, sin_t = cos_buf[turn], sin_buf[turn]
        spot = pl.multiple_of(piece * BLK, BLK)
        keys = count * BLK
        first = piece - (count - 1)
        base = pl.multiple_of(first * BLK, BLK)
        below = lax.broadcasted_iota(jnp.int32, (BLK, BLK), 0) >= lax.broadcasted_iota(jnp.int32, (BLK, BLK), 1)
        window = jnp.where(layer == 0, float(WINDOW), 65536.0)
        q_low = qp_buf[turn] - window
        totals = {}

        def rotate(raw):
            wide = raw.astype(BF).astype(F32)
            one, two = wide[:, :HALF], wide[:, HALF:]
            return one * cos_t - two * sin_t, two * cos_t + one * sin_t

        def key_value():
            normed = a_buf[...]
            one, two = rotate(dot(normed, w_qkv[layer, :, 1024:1280]))
            k_buf[stream, layer, pl.ds(spot, BLK), :HALF] = one.astype(BF)
            k_buf[stream, layer, pl.ds(spot, BLK), HALF:] = two.astype(BF)
            v_buf[stream, layer, pl.ds(spot, BLK), :] = dot(normed, w_qkv[layer, :, 1280:1536]).astype(BF)

        def query(head):
            one, two = rotate(dot(a_buf[...], w_qkv[layer, :, head * HD : (head + 1) * HD]))
            q_buf[head, :, :HALF] = (one * HD**-0.5).astype(BF)
            q_buf[head, :, HALF:] = (two * HD**-0.5).astype(BF)

        def score(head, j):
            key = k_buf[stream, layer, pl.ds(base + j * BLK, BLK), :]
            raw = lax.dot_general(q_buf[head], key, (((1,), (1,)), ((), ())), preferred_element_type=F32)
            soft = jnp.exp2(jnp.tanh(raw * (1.0 / SOFT_CAP)) * (SOFT_CAP * LOG2E))
            if j == count - 1:
                soft = jnp.where(below, soft, 0.0)
            elif count < NCP:
                k_pos = positions_of(first + j, row)
                halves = []
                for lo in (0, 128):
                    halves.append(jnp.where(q_low < k_pos[:, lo : lo + 128], soft[:, lo : lo + 128], 0.0))
                soft = jnp.concatenate(halves, axis=1)
            e_buf[head, :, j * BLK : (j + 1) * BLK] = soft
            part = soft[:, :128] + soft[:, 128:]
            totals[head] = part if j == 0 else totals[head] + part
            if j == count - 1:
                totals[head] = 1.0 / jnp.sum(totals[head], axis=-1, keepdims=True)

        def mix(head):
            prob = (e_buf[head, :, 0:keys] * totals[head]).astype(BF)
            mixed = dot(prob, v_buf[stream, layer, pl.ds(base, keys), :])
            o_buf[stream, :, head * HD : (head + 1) * HD] = mixed.astype(BF)

        return key_value, query, score, mix

    def finish(k):
        stream, layer, piece, row = unit(k)
        kept = {}

        def project(lo):
            t_buf[:, lo : lo + NCH[lo]] = dot(o_buf[stream], w_o[layer, :, lo : lo + NCH[lo]]).astype(BF)

        def norms():
            for lo in range(0, BLK, NROW):
                delta = rms(t_buf[lo : lo + NROW, :].astype(F32), gains[layer * 4 + 1])
                part = x_buf[row * NCP + piece, lo : lo + NROW, :].astype(F32)
                mid = (part + delta.astype(F32)).astype(BF)
                mid_buf[lo : lo + NROW, :] = mid
                m_buf[lo : lo + NROW, :] = rms(mid.astype(F32), gains[layer * 4 + 2])

        def mlp(lo):
            normed_mid = m_buf[...]
            gate = dot(normed_mid, w_gu[layer, :, lo : lo + FCH]).astype(BF).astype(F32)
            up = dot(normed_mid, w_gu[layer, :, FFN + lo : FFN + lo + FCH]).astype(BF).astype(F32)
            inner = gate * (0.7978845608028654 + (0.7978845608028654 * 0.044715) * (gate * gate))
            h_buf[:, lo : lo + FCH] = ((0.5 * gate) * (1.0 + jnp.tanh(inner)) * up).astype(BF)

        def down(lo):
            d_buf[:, lo : lo + NCH[lo]] = dot(h_buf[...], w_d[layer, :, lo : lo + NCH[lo]]).astype(BF)

        return project, norms, mlp, down

    def last(k):
        _, layer, piece, row = unit(jnp.maximum(k, 0))
        slot = jnp.where(k < 0, ROWS * NCP, row * NCP + piece)
        for lo in range(0, BLK, NROW):
            delta = rms(d_buf[lo : lo + NROW, :].astype(F32), gains[layer * 4 + 3])
            part = mid_buf[lo : lo + NROW, :].astype(F32)
            x_buf[slot, lo : lo + NROW, :] = (part + delta.astype(F32)).astype(BF)

    def attend_alone(k, count):
        key_value, query, score, mix = attend(k, count)
        key_value()
        for head in range(HEADS):
            query(head)
        for head in range(HEADS):
            for j in range(count):
                score(head, j)
        for head in range(HEADS):
            mix(head)

    def finish_alone(k):
        project, norms, mlp, down = finish(k)
        for lo in NCH:
            project(lo)
        norms()
        for lo in range(0, FFN, FCH):
            mlp(lo)
        for lo in NCH:
            down(lo)

    def together(k, count):
        key_value, query, score, mix = attend(k + 1, count)
        project, norms, mlp, down = finish(k)
        stream, layer, _, _ = unit(k + 1)
        for lo in NCH:
            project(lo)
        last(k - 1)
        enter(k + 1)
        rope(stream, (k + 1) // 4 + 1, layer)
        norms()
        key_value()
        for head in range(HEADS):
            query(head)
        softmax = []
        for head in range(HEADS):
            softmax += [functools.partial(score, head, j) for j in range(count)]
            if head > 0:
                softmax.append(functools.partial(mix, head - 1))
        softmax.append(functools.partial(mix, HEADS - 1))
        dense = [functools.partial(mlp, lo) for lo in range(0, FFN, FCH)] + [functools.partial(down, lo) for lo in NCH]
        order = [((i + 0.5) / len(softmax), f) for i, f in enumerate(softmax)]
        order += [((i + 0.5) / len(dense), f) for i, f in enumerate(dense)]
        for _, stage in sorted(order, key=lambda pair: pair[0]):
            stage()

    def hand_back(k):
        _, layer, piece, row = unit(k)

        @pl.when((layer == 1) & (piece == me))
        def _():
            own_out(row).start()

        @pl.when((layer == 1) & (piece != me))
        def _():
            send_out(row, piece).start()

    d_buf[...] = jnp.zeros((BLK, DIM), BF)
    mid_buf[...] = jnp.zeros((BLK, DIM), BF)
    for stream in range(2):
        for half in range(2):
            rope(stream, 0, half)
    rope(0, 1, 0)
    for copy in weight_copies(0)[:3]:
        copy.wait()
    receive(0)
    enter(0)
    attend_alone(0, 1)
    for copy in weight_copies(0)[3:]:
        copy.wait()

    def step(k, carry):
        after = k + 1
        stream, layer, piece, row = unit(after)

        @pl.when((k == 1) & (core == 1))
        def _():
            for r in range(2):
                send_piece(r, far_0).start()
                send_piece(r, far_1).start()

        @pl.when((piece == 1) & (layer == 0) & (row < ROWS - 2))
        def _():
            for dest in (partner, far_0, far_1):
                send_piece(row + 2, dest).start()

        @pl.when(k == 1)
        def _():
            for copy in weight_copies(1):
                copy.wait()

        @pl.when(layer == 0)
        def _():
            receive(after)

        blocks = jnp.where(layer == 0, jnp.minimum(piece, 2), piece) + 1
        for count in range(1, NCP + 1):
            @pl.when(blocks == count)
            def _():
                together(k, count)

        @pl.when(k > 0)
        def _():
            hand_back(k - 1)

        return carry

    lax.fori_loop(0, UNITS - 1, step, 0)
    last(UNITS - 2)
    hand_back(UNITS - 2)
    finish_alone(UNITS - 1)
    last(UNITS - 1)
    hand_back(UNITS - 1)

    for shift in range(1, NCP):
        other = peer(shift)
        send_pos(other).wait_send()
        for row in range(ROWS):
            send_piece(row, other).wait_send()
            send_out(row, other).wait_send()
            place = out.at[other * ROWS + row]
            pltpu.make_async_copy(place, place, out_recv.at[other * ROWS + row]).wait()
    for row in range(ROWS):
        own_out(row).wait()


def device_step(hidden, positions, *params):
    local_w, global_w = params[:11], params[11:]
    table = jnp.asarray(rope_lookup())
    hbm = pl.BlockSpec(memory_space=pltpu.HBM)
    vmem = pl.BlockSpec(memory_space=pltpu.VMEM)
    dma = pltpu.SemaphoreType.DMA
    return pl.pallas_call(
        kernel,
        out_shape=jax.ShapeDtypeStruct(hidden.shape, hidden.dtype),
        in_specs=[hbm, hbm, vmem] + [vmem] * 8 + [hbm] * 14,
        out_specs=pl.BlockSpec(memory_space=pl.ANY),
        scratch_shapes=[
            pltpu.VMEM((ROWS * NCP + 1, BLK, DIM), BF),
            pltpu.VMEM((NCP, NCP * ROWS, BLK), jnp.int32),
            pltpu.VMEM((2, DIM, QKV), BF),
            pltpu.VMEM((2, HEADS * HD, DIM), BF),
            pltpu.VMEM((2, DIM, 2 * FFN), BF),
            pltpu.VMEM((2, FFN, DIM), BF),
            pltpu.VMEM((2, 2, NCP * BLK, HD), BF),
            pltpu.VMEM((2, 2, NCP * BLK, HD), BF),
            pltpu.VMEM((HEADS, BLK, HD), BF),
            pltpu.VMEM((2, BLK, HEADS * HD), BF),
            pltpu.VMEM((HEADS, BLK, NCP * BLK), F32),
            pltpu.VMEM((BLK, FFN), BF),
            pltpu.VMEM((BLK, DIM), BF),
            pltpu.VMEM((BLK, DIM), BF),
            pltpu.VMEM((BLK, DIM), BF),
            pltpu.VMEM((BLK, DIM), BF),
            pltpu.VMEM((BLK, DIM), BF),
            pltpu.VMEM((4, BLK, HALF), F32),
            pltpu.VMEM((4, BLK, HALF), F32),
            pltpu.VMEM((4, BLK, 128), F32),
            pltpu.VMEM((8, 8, DIM), F32),
            dma((2, 7)),
            dma((ROWS, NCP)),
            dma((ROWS * NCP,)),
            dma((NCP,)),
            dma((NCP,)),
            dma((ROWS, NCP)),
            dma((NCP * ROWS,)),
        ],
        compiler_params=pltpu.CompilerParams(
            collective_id=0, has_side_effects=True, vmem_limit_bytes=67043328
        ),
        name="layers",
    )(hidden, positions, table, *local_w[7:], *global_w[7:], *local_w[:7], *global_w[:7])


def solution(mesh):
    specs_in = tuple([P("dp", "cp"), P("dp", "cp")] + [P()] * 22)
    return jax.shard_map(device_step, mesh=mesh, in_specs=specs_in, out_specs=P("dp", "cp"), check_vma=False)
```

time: 227 us -> 194 us (0.85)
  Pallas kernels: 213 us -> 188 us
  local copies, waits for them, and re-layouts: 12.4 us -> 5.52 us
    pallas_call x1, Pallas kernels: 213 us -> 188 us  [device_step(): pl.pallas_call(kernel, out_shape=jax.ShapeDtypeStruct(hidden.shape, hidde...]
    another operation x9 -> x0, local copies, waits for them, and re-layouts: 5.55 us -> none  [device_step(): gains = 1.0 + jnp.stack([*local_w[7:], *global_w[7:]])]
where the time goes in v2:
time: 194 us
  Pallas kernels  188 us (97%)
  local copies, waits for them, and re-layouts  5.52 us (3%)
    pallas_call x1, Pallas kernels, device_step(): pl.pallas_call(kernel, out_shape=jax.ShapeDtypeStruct(hidden.shape, hidde...  188 us
    unnamed x1, local copies, waits for them, and re-layouts  5.52 us

profile of v2, /device:TPU:3, one launch (start us, length us, event | category | flops | bytes accessed | tf_op | source)
XLA Modules:
  0.0 193.7 jit_solution(13609577539994511046)
XLA Ops:
  0.0 188.1 %layers.1 = bf16[16,256,640]{2,1,0:T(8,128)(2,1)} custom-call(bf16[16,256,640]{2,1,0:T(8,128)(2,1)} %hid.1, s32[16,256]{1,0:T(8,128)} %pos.1, bf16[384,512]{1,0:T(8,128)(2,1)} %constant.2.clone.table, f32[640]{0:T(1024)} %rest_0_.1, f32[640]{0:T(1024)} %rest_1_.1, f32[640]{0:T(1024)} %rest_2_.1, f32[640]{0:T(1024)} %rest_3_.1, f32[640]{0:T(1024)} %rest_4_.1, ...), custom_call_target="tpu_custom_call" | custom-call | tf_op jit(solution)/shard_map/layers/pallas_call | solution.py:427
  188.2 5.5 %copy.27 = bf16[16,256,640]{2,1,0:T(8,128)(2,1)} copy(bf16[16,256,640]{2,1,0:T(8,128)(2,1)} %layers.1) | data formatting | bytes 10485760

commit v3 on v2

--- a/solution.py
+++ b/solution.py
@@ -210,7 +210,7 @@
         keys = count * BLK
         first = piece - (count - 1)
         base = pl.multiple_of(first * BLK, BLK)
-        below = lax.broadcasted_iota(jnp.int32, (BLK, BLK), 0) >= lax.broadcasted_iota(jnp.int32, (BLK, BLK), 1)
+        below = lax.broadcasted_iota(jnp.int32, (128, 128), 0) >= lax.broadcasted_iota(jnp.int32, (128, 128), 1)
         window = jnp.where(layer == 0, float(WINDOW), 65536.0)
         q_low = qp_buf[turn] - window
         totals = {}
@@ -232,20 +232,31 @@
             q_buf[head, :, :HALF] = (one * HD**-0.5).astype(BF)
             q_buf[head, :, HALF:] = (two * HD**-0.5).astype(BF)
 
+        def weigh(raw):
+            return jnp.exp2(jnp.tanh(raw * (1.0 / SOFT_CAP)) * (SOFT_CAP * LOG2E))
+
         def score(head, j):
             key = k_buf[stream, layer, pl.ds(base + j * BLK, BLK), :]
             raw = lax.dot_general(q_buf[head], key, (((1,), (1,)), ((), ())), preferred_element_type=F32)
-            soft = jnp.exp2(jnp.tanh(raw * (1.0 / SOFT_CAP)) * (SOFT_CAP * LOG2E))
             if j == count - 1:
-                soft = jnp.where(below, soft, 0.0)
-            elif count < NCP:
-                k_pos = positions_of(first + j, row)
-                halves = []
-                for lo in (0, 128):
-                    halves.append(jnp.where(q_low < k_pos[:, lo : lo + 128], soft[:, lo : lo + 128], 0.0))
-                soft = jnp.concatenate(halves, axis=1)
-            e_buf[head, :, j * BLK : (j + 1) * BLK] = soft
-            part = soft[:, :128] + soft[:, 128:]
+                early = jnp.where(below, weigh(raw[:128, :128]), 0.0)
+                late = weigh(raw[128:, :128])
+                rest = jnp.where(below, weigh(raw[128:, 128:]), 0.0)
+                e_buf[head, :128, j * BLK : j * BLK + 128] = early
+                e_buf[head, 128:, j * BLK : j * BLK + 128] = late
+                e_buf[head, :128, j * BLK + 128 : (j + 1) * BLK] = jnp.zeros((128, 128), F32)
+                e_buf[head, 128:, j * BLK + 128 : (j + 1) * BLK] = rest
+                part = jnp.concatenate([early, late + rest], axis=0)
+            else:
+                soft = weigh(raw)
+                if count < NCP:
+                    k_pos = positions_of(first + j, row)
+                    halves = []
+                    for lo in (0, 128):
+                        halves.append(jnp.where(q_low < k_pos[:, lo : lo + 128], soft[:, lo : lo + 128], 0.0))
+                    soft = jnp.concatenate(halves, axis=1)
+                e_buf[head, :, j * BLK : (j + 1) * BLK] = soft
+                part = soft[:, :128] + soft[:, 128:]
             totals[head] = part if j == 0 else totals[head] + part
             if j == count - 1:
                 totals[head] = 1.0 / jnp.sum(totals[head], axis=-1, keepdims=True)
@@ -424,7 +435,7 @@
     hbm = pl.BlockSpec(memory_space=pltpu.HBM)
     vmem = pl.BlockSpec(memory_space=pltpu.VMEM)
     dma = pltpu.SemaphoreType.DMA
-    return pl.pallas_call(
+    mixed = pl.pallas_call(
         kernel,
         out_shape=jax.ShapeDtypeStruct(hidden.shape, hidden.dtype),
         in_specs=[hbm, hbm, vmem] + [vmem] * 8 + [hbm] * 14,
@@ -464,6 +475,15 @@
         ),
         name="layers",
     )(hidden, positions, table, *local_w[7:], *global_w[7:], *local_w[:7], *global_w[:7])
+    tile = pl.BlockSpec((2, BLK, DIM), lambda i: (i, 0, 0))
+    return pl.pallas_call(
+        lambda src, dst: dst.__setitem__(..., src[...]),
+        out_shape=jax.ShapeDtypeStruct(hidden.shape, hidden.dtype),
+        grid=(hidden.shape[0] // 2,),
+        in_specs=[tile],
+        out_specs=tile,
+        name="settle",
+    )(mixed)
 
 
 def solution(mesh):

time: 194 us -> 196 us (1.010)
  Pallas kernels: 188 us -> 195 us
  local copies, waits for them, and re-layouts: 5.52 us -> 0 us
    pallas_call x0 -> x1, Pallas kernels: none -> 7.26 us  [device_step(): pl.pallas_call(lambda src, dst: dst.__setitem__(..., src[...]), out_shape...]
    unnamed x1 -> x0, local copies, waits for them, and re-layouts: 5.52 us -> none
where the time goes in v3:
time: 196 us; the launch traced here: 195 us
  Pallas kernels  195 us (99%)
    pallas_call x1, Pallas kernels, device_step(): pl.pallas_call(kernel, out_shape=jax.ShapeDtypeStruct(hidden.shape, hidde...  188 us
    pallas_call x1, Pallas kernels, device_step(): pl.pallas_call(lambda src, dst: dst.__setitem__(..., src[...]), out_shape...  7.26 us

profile of v3, /device:TPU:3, one launch (start us, length us, event | category | flops | bytes accessed | tf_op | source)
XLA Modules:
  0.0 195.3 jit_solution(3804680319686161938)
XLA Ops:
  0.0 188.1 %layers.1.src = bf16[16,256,640]{2,1,0:T(8,128)(2,1)} custom-call(bf16[16,256,640]{2,1,0:T(8,128)(2,1)} %hid.1, s32[16,256]{1,0:T(8,128)} %pos.1, bf16[384,512]{1,0:T(8,128)(2,1)} %constant.2.clone.table, f32[640]{0:T(1024)} %rest_0_.1, f32[640]{0:T(1024)} %rest_1_.1, f32[640]{0:T(1024)} %rest_2_.1, f32[640]{0:T(1024)} %rest_3_.1, f32[640]{0:T(1024)} %rest_4_.1, ...), custom_call_target="tpu_custom_call" | custom-call | tf_op jit(solution)/shard_map/layers/pallas_call | solution.py:438
  188.1 7.3 %settle.1 = bf16[16,256,640]{2,1,0:T(8,128)(2,1)} custom-call(bf16[16,256,640]{2,1,0:T(8,128)(2,1)} %layers.1.src), custom_call_target="tpu_custom_call" | custom-call | tf_op jit(solution)/shard_map/settle/pallas_call | solution.py:479

commit v4 on v3

--- a/solution.py
+++ b/solution.py
@@ -365,18 +365,20 @@
     for stream in range(2):
         for half in range(2):
             rope(stream, 0, half)
-    rope(0, 1, 0)
     for copy in weight_copies(0)[:3]:
-        copy.wait()
-    receive(0)
-    enter(0)
-    attend_alone(0, 1)
-    for copy in weight_copies(0)[3:]:
         copy.wait()
 
     def step(k, carry):
         after = k + 1
         stream, layer, piece, row = unit(after)
+        alone = (k == 0) & (me >= 2)
+        opening = k < 0
+        closing = k == UNITS - 1
+
+        @pl.when(k == 0)
+        def _():
+            for copy in weight_copies(0)[3:]:
+                copy.wait()
 
         @pl.when((k == 1) & (core == 1))
         def _():
@@ -394,27 +396,41 @@
             for copy in weight_copies(1):
                 copy.wait()
 
-        @pl.when(layer == 0)
+        @pl.when(alone | closing)
+        def _():
+            last(k - 1)
+
+            @pl.when(closing)
+            def _():
+                hand_back(k - 1)
+
+            finish_alone(k)
+            last(k)
+
+        @pl.when((layer == 0) & (k < UNITS - 1))
         def _():
             receive(after)
 
+        @pl.when(alone | opening)
+        def _():
+            enter(after)
+            attend_alone(after, 1)
+            rope(stream, after // 4 + 1, layer)
+
         blocks = jnp.where(layer == 0, jnp.minimum(piece, 2), piece) + 1
+        blocks = jnp.where(alone | opening | closing, 0, blocks)
         for count in range(1, NCP + 1):
             @pl.when(blocks == count)
             def _():
                 together(k, count)
 
-        @pl.when(k > 0)
+        @pl.when((k > 0) & (k < UNITS - 1))
         def _():
             hand_back(k - 1)
 
         return carry
 
-    lax.fori_loop(0, UNITS - 1, step, 0)
-    last(UNITS - 2)
-    hand_back(UNITS - 2)
-    finish_alone(UNITS - 1)
-    last(UNITS - 1)
+    lax.fori_loop(-1, UNITS, step, 0)
     hand_back(UNITS - 1)
 
     for shift in range(1, NCP):
@@ -435,7 +451,7 @@
     hbm = pl.BlockSpec(memory_space=pltpu.HBM)
     vmem = pl.BlockSpec(memory_space=pltpu.VMEM)
     dma = pltpu.SemaphoreType.DMA
-    mixed = pl.pallas_call(
+    return pl.pallas_call(
         kernel,
         out_shape=jax.ShapeDtypeStruct(hidden.shape, hidden.dtype),
         in_specs=[hbm, hbm, vmem] + [vmem] * 8 + [hbm] * 14,
@@ -475,15 +491,6 @@
         ),
         name="layers",
     )(hidden, positions, table, *local_w[7:], *global_w[7:], *local_w[:7], *global_w[:7])
-    tile = pl.BlockSpec((2, BLK, DIM), lambda i: (i, 0, 0))
-    return pl.pallas_call(
-        lambda src, dst: dst.__setitem__(..., src[...]),
-        out_shape=jax.ShapeDtypeStruct(hidden.shape, hidden.dtype),
-        grid=(hidden.shape[0] // 2,),
-        in_specs=[tile],
-        out_specs=tile,
-        name="settle",
-    )(mixed)
 
 
 def solution(mesh):

time: 196 us -> 192 us (0.980)
  Pallas kernels: 195 us -> 186 us
  local copies, waits for them, and re-layouts: 0 us -> 5.52 us
    pallas_call x1 -> x0, Pallas kernels: 7.26 us -> none  [device_step(): pl.pallas_call(lambda src, dst: dst.__setitem__(..., src[...]), out_shape...]
    unnamed x0 -> x1, local copies, waits for them, and re-layouts: none -> 5.52 us
    pallas_call x1, Pallas kernels: 188 us -> 186 us  [device_step(): pl.pallas_call(kernel, out_shape=jax.ShapeDtypeStruct(hidden.shape, hidde...]
where the time goes in v4:
time: 192 us; the launch traced here: 191 us
  Pallas kernels  186 us (97%)
  local copies, waits for them, and re-layouts  5.52 us (3%)
    pallas_call x1, Pallas kernels, device_step(): pl.pallas_call(kernel, out_shape=jax.ShapeDtypeStruct(hidden.shape, hidde...  186 us
    unnamed x1, local copies, waits for them, and re-layouts  5.52 us

profile of v4, /device:TPU:3, one launch (start us, length us, event | category | flops | bytes accessed | tf_op | source)
XLA Modules:
  0.0 191.3 jit_solution(5495828823580680011)
XLA Ops:
  0.0 185.8 %layers.1 = bf16[16,256,640]{2,1,0:T(8,128)(2,1)} custom-call(bf16[16,256,640]{2,1,0:T(8,128)(2,1)} %hid.1, s32[16,256]{1,0:T(8,128)} %pos.1, bf16[384,512]{1,0:T(8,128)(2,1)} %constant.2.clone.table, f32[640]{0:T(1024)} %rest_0_.1, f32[640]{0:T(1024)} %rest_1_.1, f32[640]{0:T(1024)} %rest_2_.1, f32[640]{0:T(1024)} %rest_3_.1, f32[640]{0:T(1024)} %rest_4_.1, ...), custom_call_target="tpu_custom_call" | custom-call | tf_op jit(solution)/shard_map/layers/pallas_call | solution.py:454
  185.8 5.5 %copy.27 = bf16[16,256,640]{2,1,0:T(8,128)(2,1)} copy(bf16[16,256,640]{2,1,0:T(8,128)(2,1)} %layers.1) | data formatting | bytes 10485760

commit v5 on v4

--- a/solution.py
+++ b/solution.py
@@ -23,7 +23,7 @@
 ROWS = 4
 UNITS = ROWS * NCP * 2
 QKV = HEADS * HD + 2 * HD
-FCH = 256
+FCH = 512
 NROW = 64
 NCH = {0: 256, 256: 256, 512: 128}
 LOW = 64
@@ -372,6 +372,7 @@
         after = k + 1
         stream, layer, piece, row = unit(after)
         alone = (k == 0) & (me >= 2)
+        early = (k == UNITS - 2) & (me < 2)
         opening = k < 0
         closing = k == UNITS - 1
 
@@ -396,16 +397,22 @@
             for copy in weight_copies(1):
                 copy.wait()
 
-        @pl.when(alone | closing)
-        def _():
-            last(k - 1)
-
-            @pl.when(closing)
+        @pl.when(alone | early | closing)
+        def _():
+            @pl.when(alone | early | (me >= 2))
+            def _():
+                last(k - 1)
+
+            @pl.when(closing & (me >= 2))
             def _():
                 hand_back(k - 1)
 
             finish_alone(k)
             last(k)
+
+            @pl.when(early)
+            def _():
+                hand_back(k)
 
         @pl.when((layer == 0) & (k < UNITS - 1))
         def _():
@@ -417,8 +424,13 @@
             attend_alone(after, 1)
             rope(stream, after // 4 + 1, layer)
 
+        @pl.when(early)
+        def _():
+            enter(after)
+            attend_alone(after, NCP)
+
         blocks = jnp.where(layer == 0, jnp.minimum(piece, 2), piece) + 1
-        blocks = jnp.where(alone | opening | closing, 0, blocks)
+        blocks = jnp.where(alone | early | opening | closing, 0, blocks)
         for count in range(1, NCP + 1):
             @pl.when(blocks == count)
             def _():

time: 192 us -> 190 us (0.990)
  Pallas kernels: 186 us -> 184 us
where the time goes in v5:
time: 190 us
  Pallas kernels  184 us (97%)
  local copies, waits for them, and re-layouts  5.52 us (3%)
    pallas_call x1, Pallas kernels, device_step(): pl.pallas_call(kernel, out_shape=jax.ShapeDtypeStruct(hidden.shape, hidde...  184 us
    unnamed x1, local copies, waits for them, and re-layouts  5.52 us

profile of v5, /device:TPU:3, one launch (start us, length us, event | category | flops | bytes accessed | tf_op | source)
XLA Modules:
  0.0 189.6 jit_solution(13135493964439887160)
XLA Ops:
  0.0 184.1 %layers.1 = bf16[16,256,640]{2,1,0:T(8,128)(2,1)} custom-call(bf16[16,256,640]{2,1,0:T(8,128)(2,1)} %hid.1, s32[16,256]{1,0:T(8,128)} %pos.1, bf16[384,512]{1,0:T(8,128)(2,1)} %constant.2.clone.table, f32[640]{0:T(1024)} %rest_0_.1, f32[640]{0:T(1024)} %rest_1_.1, f32[640]{0:T(1024)} %rest_2_.1, f32[640]{0:T(1024)} %rest_3_.1, f32[640]{0:T(1024)} %rest_4_.1, ...), custom_call_target="tpu_custom_call" | custom-call | tf_op jit(solution)/shard_map/layers/pallas_call | solution.py:466
  184.1 5.5 %copy.27 = bf16[16,256,640]{2,1,0:T(8,128)(2,1)} copy(bf16[16,256,640]{2,1,0:T(8,128)(2,1)} %layers.1) | data formatting | bytes 10485760
